TPU v7x, 32 devices: a whole 2x2x4 slice. The times are simulated.
32 devices in a mesh: parts: 2 (over y), sub: 4 (over z), row: 2 (over x), col: 2 (over core).
Axes of the slice: x: 2, y: 2, z: 4, core: 2. Of those that a mesh axis runs over, the one named last changes fastest.
Arguments:
- loads: float32 [8, 32, 1024], P(('parts', 'sub'), 'col'), parts along dimension 0, may hold values from -6 to 6
- weights: float32 [8, 1024], P(('parts', 'sub')), parts along dimension 0, may hold values from 0.25 to 4
- dual_ops: bfloat16 [8, 2048, 2048], P(('parts', 'sub'), 'row'), parts along dimension 0, as said below
- corner_maps: bfloat16 [8, 24, 2048], P(('parts', 'sub'), None, 'row'), parts along dimension 0, may hold values from -0.25 to 0.25
- coarse_inverse: float32 [96, 48], P('parts'), parts along dimension 0, as said below
- corner_ids: int32 [8, 24], P('parts'), parts along dimension 0, may hold values from 0 to 47, as said below
- iface_sizes: int32 [8], P('parts'), parts along dimension 0, may hold values from 512 to 1024, as said below
- left_partner: int32 [8, 1024], P(('parts', 'sub')), parts along dimension 0, may hold values from 0 to 1023, as said below
- right_partner: int32 [8, 1024], P(('parts', 'sub')), parts along dimension 0, may hold values from 0 to 1023, as said below
Outputs:
- solution: float32 [8, 32, 1024], P(('parts', 'sub'), 'col'), parts along dimension 0
- residual: float32 [8, 32, 1024], P(('parts', 'sub'), 'col'), parts along dimension 0
There are 2 independent parts, one for each index of `parts`. A program takes and returns all parts, laid end to end along the dimension named above; each array names one. Nothing has to cross between parts.
Inputs may be any that keep to these rules, and one draw needn't show every extreme that they name: Global indices 24/2 * s to 24/2 * s + 24/2 - 1 are the corners of the interface between s and s+1; the first half of subdomain s's corner_ids is a permutation of those of interface s-1, the second half a permutation of those of interface s. `left_partner`: each row s is a permutation that maps the slots below iface_sizes[s-1] onto slots below it. `right_partner`: each row s is a permutation that maps the slots below iface_sizes[s] onto slots below it, and is the inverse of left_partner[s+1]. `dual_ops`: symmetric positive definite. `coarse_inverse`: symmetric positive definite. For each s < 2, one of iface_sizes[s] and iface_sizes[s + 2] is 896 or more and the other 640 or less.
All inputs are finite; a program needn't handle non-finite values.
Results may differ from a plain program's by a relative error of at most 0.015.
Values may be sent and summed in bfloat16 or wider, within the bound.
A program may use at most 64 MiB of HBM per device.

v0:
```python
import functools

import jax
import jax.numpy as jnp
from jax import lax
from jax.experimental import pallas as pl
from jax.experimental.pallas import tpu as pltpu
from jax.sharding import PartitionSpec as P

MESH = pl.DeviceIdType.MESH
CHUNK = 256
BF = jnp.bfloat16
F32 = jnp.float32


def each(count, body):
    if count <= 8:
        for at in range(count):
            body(at)
    else:
        lax.fori_loop(0, count, lambda at, _: (body(at), 0)[1], 0)


def dot_nt(a, b):
    return lax.dot_general(a, b, (((1,), (1,)), ((), ())), preferred_element_type=F32)


def dot_nn(a, b):
    return lax.dot_general(a, b, (((1,), (0,)), ((), ())), preferred_element_type=F32)


def kernel(
    S, R, loads, weights, op, cm, cinv, ids, sizes, lmap, rmap, sol, res,
    loads_v, w_v, op_v, cv, cinv_p, ids_v, lmap_v, rmap_v,
    zsend, zrecv, wrecv, cmo, cmn, mo, mn, pl_m, pr_m, zs,
    own, nbr, pk,
    in_sem, op_sem, z_sem, cmo_ssem, cmo_rsem, cmn_ssem, cmn_rsem,
    own_ssem, own_rsem, nbr_ssem, nbr_rsem, pk_ssem, pk_rsem,
):
    s = lax.axis_index("sub")
    r = lax.axis_index("row")
    G = S * R
    me = s * R + r
    C, H = loads_v.shape
    B = op_v.shape[0]
    NC = cv.shape[0]
    W = cinv_p.shape[0]
    half_r = R // 2
    nxt = lax.rem(s + 1, S)
    prv = lax.rem(s + S - 1, S)
    side = r // half_r
    toward = lax.rem(s + S - 1 + 2 * side, S)

    ins = [
        pltpu.make_async_copy(src, dst, in_sem.at[i])
        for i, (src, dst) in enumerate([
            (loads.at[0], loads_v), (weights, w_v), (rmap, rmap_v), (lmap, lmap_v),
            (ids, ids_v), (cinv, cv), (cm.at[0], cmo.at[r]),
        ])
    ]
    for copy in ins:
        copy.start()
    chunk = min(CHUNK, B)
    ops = [
        pltpu.make_async_copy(
            op.at[0, pl.ds(c * chunk, chunk), :], op_v.at[pl.ds(c * chunk, chunk), :], op_sem.at[c]
        )
        for c in range(B // chunk)
    ]
    for copy in ops:
        copy.start()

    barrier = pltpu.get_barrier_semaphore()

    def peer(k):
        g = lax.rem(me + k + 1, G)
        return g, {"sub": g // R, "row": lax.rem(g, R)}

    def greet(k):
        _, who = peer(k)
        pl.semaphore_signal(barrier, inc=1, device_id=who, device_id_type=MESH)

    each(G - 1, greet)

    size_before = sizes[prv]
    size_after = sizes[s]
    lanes = lax.broadcasted_iota(jnp.int32, (1, H), 1)
    live_l = (lanes < size_before).astype(F32)
    ins[0].wait()
    ins[1].wait()
    w_l = w_v[...]
    r0 = loads_v[...] * live_l
    z0 = w_l * r0
    zsend[...] = z0.astype(BF)

    pl.semaphore_wait(barrier, G - 1)

    def remote(src, dst, ssem, rsem, who):
        return pltpu.make_async_remote_copy(
            src_ref=src, dst_ref=dst, send_sem=ssem, recv_sem=rsem, device_id=who, device_id_type=MESH
        )

    z_copy = remote(zsend, zrecv, z_sem.at[0], z_sem.at[1], {"sub": prv})
    w_copy = remote(weights, wrecv, z_sem.at[2], z_sem.at[3], {"sub": prv})
    z_copy.start()
    w_copy.start()

    def to_row(src, dst, ssem, rsem, k):
        q = lax.rem(r + k, R)
        return remote(src, dst.at[r], ssem.at[k], rsem.at[r], {"row": q})

    def to_side(src, dst, ssem, rsem, k):
        q = lax.rem(r + k, R)
        return remote(src, dst.at[r], ssem.at[k], rsem.at[r], {"sub": toward, "row": q})

    def wait_slot(dst, ssem, rsem, q):
        remote(dst.at[q], dst.at[q], ssem.at[0], rsem.at[q], {"sub": nxt}).wait_recv()

    cm_sends = [to_row(cm.at[0], cmo, cmo_ssem, cmo_rsem, k) for k in range(1, R)]
    cm_sends += [to_side(cm.at[0], cmn, cmn_ssem, cmn_rsem, k) for k in range(R)]
    for copy in cm_sends:
        copy.start()

    ins[2].wait()
    ins[3].wait()
    right_map = rmap_v[...]
    left_map = lmap_v[...]
    live_r = (right_map < size_after).astype(F32)

    def hot(target, the_map):
        step = 128
        for c in range(H // step):
            rows = lax.broadcasted_iota(jnp.int32, (step, H), 0) + c * step
            target[pl.ds(c * step, step), :] = (rows == the_map).astype(F32).astype(BF)

    hot(pr_m, right_map)
    hot(pl_m, left_map)
    ins[4].wait()
    ins[5].wait()
    cinv_p[...] = jnp.zeros_like(cinv_p)
    cinv_p[0:NC, 0:NC] = cv[...]

    def hot_ids(t):
        row = ids_v[pl.ds(t, 1), :]
        rows = lax.broadcasted_iota(jnp.int32, (W, row.shape[1]), 0)
        return (rows == row).astype(F32).astype(BF)

    hot_own = hot_ids(s)
    ins[6].wait()
    mo[r] = dot_nn(hot_own, cmo[r]).astype(BF)

    z_copy.wait_recv()
    w_copy.wait_recv()
    w_in = wrecv[...]
    w_hi = w_in.astype(BF)
    w_lo = (w_in - w_hi.astype(F32)).astype(BF)
    pad = lax.broadcasted_iota(jnp.int32, (16, H), 0)
    w_rows = jnp.where(pad == 0, w_hi.astype(F32), jnp.where(pad == 1, w_lo.astype(F32), 0.0))
    gathered = dot_nn(jnp.concatenate([zrecv[...], w_rows.astype(BF)], axis=0), pr_m[...])
    z0_r = gathered[:C]
    w_r = gathered[C : C + 1] + gathered[C + 1 : C + 2]

    col = lax.broadcasted_iota(jnp.int32, (C, W), 1)

    def pick(value, lane):
        return jnp.sum(jnp.where(col == lane, value, 0.0), axis=1, keepdims=True)

    def product(step, z_left, z_right, r_left):
        full = jnp.concatenate([z_left.astype(BF), z_right.astype(BF)], axis=1)
        for q in range(R):
            half = z_left if q < half_r else z_right
            at = (q % half_r) * B
            zs[q] = half[:, at : at + B]
        parts = []
        for c in range(B // chunk):
            if step == 0:
                ops[c].wait()
            parts.append(dot_nt(full, op_v[c * chunk : (c + 1) * chunk, :]))
        local = jnp.concatenate(parts, axis=1)
        own[step, r] = local.astype(BF)
        mine = own.at[step, r]
        sends = [
            to_side(mine, nbr.at[step], nbr_ssem.at[step], nbr_rsem.at[step], k) for k in range(R)
        ]
        sends += [
            to_row(mine, own.at[step], own_ssem.at[step], own_rsem.at[step], k) for k in range(1, R)
        ]
        for copy in sends:
            copy.start()
        block = zs[r]
        delta = jnp.sum(block * local, axis=1, keepdims=True)
        gamma = jnp.sum(r_left * z_left, axis=1, keepdims=True)
        gamma = jnp.where(r == 0, gamma, 0.0)
        corner = dot_nt(block.astype(BF), mo[r])
        packet = corner + jnp.where(col == NC, gamma, 0.0) + jnp.where(col == NC + 1, delta, 0.0)
        pk[step, me] = packet

        def spread(k):
            _, who = peer(k)
            remote(
                pk.at[step, me], pk.at[step, me], pk_ssem.at[step, k], pk_rsem.at[step, me], who
            ).start()

        each(G - 1, spread)
        return sends

    def collect(step, need_right):
        def arrive(k):
            g, who = peer(k)
            remote(
                pk.at[step, g], pk.at[step, g], pk_ssem.at[step, 0], pk_rsem.at[step, g], who
            ).wait_recv()

        each(G - 1, arrive)
        if G <= 8:
            total = pk[step, 0]
            for g in range(1, G):
                total = total + pk[step, g]
        else:
            total = lax.fori_loop(
                0, G, lambda g, acc: acc + pk[step, g], jnp.zeros((C, W), F32)
            )
        solved = lax.dot_general(
            total, cinv_p[...], (((1,), (0,)), ((), ())),
            precision=lax.Precision.HIGHEST, preferred_element_type=F32,
        )
        back = solved.astype(BF)
        gamma = pick(total, NC)
        delta = pick(total, NC + 1) + jnp.sum(total * back.astype(F32), axis=1, keepdims=True)
        for k in range(1, R):
            wait_slot(own.at[step], own_ssem.at[step], own_rsem.at[step], lax.rem(r + k, R))
        for q in range(R):
            wait_slot(nbr.at[step], nbr_ssem.at[step], nbr_rsem.at[step], q)

        def joined(store, maps, first, last):
            return jnp.concatenate(
                [store[step, q].astype(F32) + dot_nn(back, maps[q]) for q in range(first, last)], axis=1
            )

        from_prev = joined(nbr, mn, half_r, R).astype(BF)
        w_left = (joined(own, mo, 0, half_r) + dot_nn(from_prev, pl_m[...])) * live_l
        w_right = None
        if need_right:
            from_next = joined(nbr, mn, 0, half_r).astype(BF)
            w_right = (joined(own, mo, half_r, R) + dot_nn(from_next, pr_m[...])) * live_r
        return gamma, delta, w_left, w_right

    sends0 = product(0, z0, z0_r, r0)

    for k in range(1, R):
        q = lax.rem(r + k, R)
        wait_slot(cmo, cmo_ssem, cmo_rsem, q)
        mo[q] = dot_nn(hot_own, cmo[q]).astype(BF)
    hot_next = hot_ids(nxt)
    hot_prev = hot_ids(prv)
    for q in range(R):
        wait_slot(cmn, cmn_ssem, cmn_rsem, q)
        mn[q] = dot_nn(hot_next if q < half_r else hot_prev, cmn[q]).astype(BF)

    gamma0, delta0, wl0, wr0 = collect(0, True)
    alpha0 = gamma0 / delta0
    r1 = r0 - alpha0 * wl0
    z1 = w_l * r1
    z1_r = z0_r - alpha0 * (w_r * wr0)
    sends1 = product(1, z1, z1_r, r1)
    gamma1, delta1, wl1, _ = collect(1, False)
    beta = gamma1 / gamma0
    alpha1 = gamma1 / (delta1 - beta * gamma1 / alpha0)
    sol[...] = alpha0 * z0 + alpha1 * (z1 + beta * z0)
    res[...] = r1 - alpha1 * (wl1 + beta * wl0)

    z_copy.wait_send()
    w_copy.wait_send()
    for copy in cm_sends + sends0 + sends1:
        copy.wait_send()
    for step in range(2):

        def drain(k):
            _, who = peer(k)
            remote(
                pk.at[step, me], pk.at[step, me], pk_ssem.at[step, k], pk_rsem.at[step, me], who
            ).wait_send()

        each(G - 1, drain)


def per_device(S, R, loads, weights, dual_ops, corner_maps, coarse_inverse, corner_ids,
               iface_sizes, left_partner, right_partner):
    _, C, H = loads.shape
    _, B, full = dual_ops.shape
    J = corner_maps.shape[1]
    NC = coarse_inverse.shape[0]
    W = (NC + 2 + 127) // 128 * 128
    G = S * R
    DMA = pltpu.SemaphoreType.DMA
    anywhere = pl.BlockSpec(memory_space=pltpu.HBM)
    vmem = pl.BlockSpec(memory_space=pltpu.VMEM)
    out = jax.ShapeDtypeStruct((C, H), F32)
    sol, res = pl.pallas_call(
        functools.partial(kernel, S, R),
        out_shape=(out, out),
        in_specs=[anywhere] * 6 + [pl.BlockSpec(memory_space=pltpu.SMEM)] + [anywhere] * 2,
        out_specs=(vmem, vmem),
        scratch_shapes=[
            pltpu.VMEM((C, H), F32), pltpu.VMEM((1, H), F32), pltpu.VMEM((B, full), BF),
            pltpu.VMEM((NC, NC), F32), pltpu.VMEM((W, W), F32), pltpu.VMEM(corner_ids.shape, jnp.int32),
            pltpu.VMEM((1, H), jnp.int32), pltpu.VMEM((1, H), jnp.int32),
            pltpu.VMEM((C, H), BF), pltpu.VMEM((C, H), BF), pltpu.VMEM((1, H), F32),
            pltpu.VMEM((R, J, B), BF), pltpu.VMEM((R, J, B), BF),
            pltpu.VMEM((R, W, B), BF), pltpu.VMEM((R, W, B), BF),
            pltpu.VMEM((H, H), BF), pltpu.VMEM((H, H), BF), pltpu.VMEM((R, C, B), F32),
            pltpu.VMEM((2, R, C, B), BF), pltpu.VMEM((2, R, C, B), BF), pltpu.VMEM((2, G, C, W), F32),
            DMA((7,)), DMA((B // min(CHUNK, B),)), DMA((4,)), DMA((R,)), DMA((R,)), DMA((R,)), DMA((R,)),
            DMA((2, R)), DMA((2, R)), DMA((2, R)), DMA((2, R)), DMA((2, G)), DMA((2, G)),
        ],
        compiler_params=pltpu.CompilerParams(
            collective_id=0, has_side_effects=True, vmem_limit_bytes=67_043_328
        ),
    )(loads, weights, dual_ops, corner_maps, coarse_inverse, corner_ids, iface_sizes,
      left_partner, right_partner)
    return sol[None], res[None]


def solution(mesh):
    placed = (
        P(("parts", "sub"), "col", None),
        P(("parts", "sub"), None),
        P(("parts", "sub"), "row", None),
        P(("parts", "sub"), None, "row"),
        P("parts", None),
        P("parts", None),
        P("parts"),
        P(("parts", "sub"), None),
        P(("parts", "sub"), None),
    )
    return jax.shard_map(
        functools.partial(per_device, mesh.shape["sub"], mesh.shape["row"]),
        mesh=mesh,
        in_specs=placed,
        out_specs=(P(("parts", "sub"), "col", None), P(("parts", "sub"), "col", None)),
        check_vma=False,
    )
```

profile of v0, /device:TPU:0, one launch (start us, length us, event | category | flops | bytes accessed | tf_op | source)
XLA Modules:
  0.0 31.0 jit_solution(5196444162923319760)
XLA Ops:
  0.6 27.4 %shard_map.104 = (f32[16,1024]{1,0:T(8,128)}, f32[16,1024]{1,0:T(8,128)}) custom-call(f32[1,16,1024]{2,1,0:T(8,128)} %loads.1, f32[1,1024]{1,0:T(1,128)} %weights.1, bf16[1,1024,2048]{2,1,0:T(8,128)(2,1)} %op.1, bf16[1,24,1024]{2,1,0:T(8,128)(2,1)} %cm.1, f32[48,48]{1,0:T(8,128)} %cinv.1, s32[4,24]{1,0:T(4,128)} %ids.1, s32[4]{0:T(128)} %sizes.1, ...), custom_call_target="tpu_custom_call" | custom-call | tf_op jit(solution)/shard_map/pallas_call | solution.py:299
  28.1 1.5 %copy.13 = f32[1,16,1024]{2,1,0:T(8,128)} copy(f32[1,16,1024]{2,1,0:T(8,128)} %bitcast.3) | data formatting | bytes 131072
  29.6 1.5 %copy.14 = f32[1,16,1024]{2,1,0:T(8,128)} copy(f32[1,16,1024]{2,1,0:T(8,128)} %bitcast.2) | data formatting | bytes 131072
where the time goes:
time: 31.3 us; the launch traced here: 31 us
  Pallas kernels  27.4 us (88%)
  local copies, waits for them, and re-layouts  2.95 us (9%)
  between operations  0.64 us (2%)
    pallas_call x1, Pallas kernels, per_device(): pl.pallas_call(functools.partial(kernel, S, R), out_shape=(out, out), in_...  27.4 us
    unnamed x2, local copies, waits for them, and re-layouts  2.95 us

commit v1 on v0

v1 whole, which is shorter than its diff:
```python
import functools

import jax
import jax.numpy as jnp
from jax import lax
from jax.experimental import pallas as pl
from jax.experimental.pallas import tpu as pltpu
from jax.sharding import PartitionSpec as P

MESH = pl.DeviceIdType.MESH
LIMIT = 40 * 2**20
BF = jnp.bfloat16
F32 = jnp.float32


def each(count, body):
    if count <= 8:
        for at in range(count):
            body(at)
    else:
        lax.fori_loop(0, count, lambda at, _: (body(at), 0)[1], 0)


def dot_nt(a, b):
    return lax.dot_general(a, b, (((1,), (1,)), ((), ())), preferred_element_type=F32)


def dot_nn(a, b):
    return lax.dot_general(a, b, (((1,), (0,)), ((), ())), preferred_element_type=F32)


def kernel(
    S, R, loads, weights, op, cm, cinv, ids, sizes, lmap, rmap, sol, res,
    loads_v, w_v, op_v, cv, cinv_p, ids_v, lmap_v, rmap_v, sizes_v,
    zsend, zrecv, wrecv, cmo, cmn, mo, mn, pl_m, pr_m, zs, acc,
    own, nbr, pk, dk,
    in_sem, op_sem, z_sem, cmo_ssem, cmo_rsem, cmn_ssem, cmn_rsem,
    own_ssem, own_rsem, nbr_ssem, nbr_rsem, pk_ssem, pk_rsem, dk_ssem, dk_rsem,
):
    s = lax.axis_index("sub")
    r = lax.axis_index("row")
    G = S * R
    me = s * R + r
    C, H = loads_v.shape
    B = op_v.shape[0]
    NC = cv.shape[0]
    W = cinv_p.shape[0]
    half_r = R // 2
    nxt = lax.rem(s + 1, S)
    prv = lax.rem(s + S - 1, S)
    side = r // half_r
    toward = lax.rem(s + S - 1 + 2 * side, S)

    barrier = pltpu.get_barrier_semaphore()

    def peer(k):
        g = lax.rem(me + k + 1, G)
        return g, {"sub": g // R, "row": lax.rem(g, R)}

    def greet(k):
        _, who = peer(k)
        pl.semaphore_signal(barrier, inc=1, device_id=who, device_id_type=MESH)

    each(G - 1, greet)

    ins = [
        pltpu.make_async_copy(src, dst, in_sem.at[i])
        for i, (src, dst) in enumerate([
            (loads.at[0], loads_v), (weights, w_v), (sizes, sizes_v), (rmap, rmap_v), (lmap, lmap_v),
            (ids, ids_v), (cinv, cv), (cm.at[0], cmo.at[r]),
        ])
    ]
    for copy in ins:
        copy.start()
    op_copy = pltpu.make_async_copy(op.at[0], op_v, op_sem)
    op_copy.start()

    for copy in ins[:3]:
        copy.wait()
    lanes = lax.broadcasted_iota(jnp.int32, (1, H), 1)
    live_l = (lanes < sizes_v[prv]).astype(F32)
    size_after = sizes_v[s]
    w_l = w_v[...]
    r0 = loads_v[...] * live_l
    z0 = w_l * r0
    zsend[...] = z0.astype(BF)

    pl.semaphore_wait(barrier, G - 1)

    def remote(src, dst, ssem, rsem, who):
        return pltpu.make_async_remote_copy(
            src_ref=src, dst_ref=dst, send_sem=ssem, recv_sem=rsem, device_id=who, device_id_type=MESH
        )

    z_copy = remote(zsend, zrecv, z_sem.at[0], z_sem.at[1], {"sub": prv})
    w_copy = remote(w_v, wrecv, z_sem.at[2], z_sem.at[3], {"sub": prv})
    z_copy.start()
    w_copy.start()

    def to_row(src, dst, ssem, rsem, k):
        q = lax.rem(r + k, R)
        return remote(src, dst.at[r], ssem.at[k], rsem.at[r], {"row": q})

    def to_side(src, dst, ssem, rsem, k):
        q = lax.rem(r + k, R)
        return remote(src, dst.at[r], ssem.at[k], rsem.at[r], {"sub": toward, "row": q})

    def wait_slot(dst, ssem, rsem, q):
        remote(dst.at[q], dst.at[q], ssem.at[0], rsem.at[q], {"sub": nxt}).wait_recv()

    cm_sends = [to_side(cm.at[0], cmn, cmn_ssem, cmn_rsem, k) for k in range(R)]
    cm_sends += [to_row(cm.at[0], cmo, cmo_ssem, cmo_rsem, k) for k in range(1, R)]

    def send_maps():
        for copy in cm_sends:
            copy.start()

    ins[3].wait()
    ins[4].wait()
    right_map = rmap_v[...]
    left_map = lmap_v[...]
    live_r = (right_map < size_after).astype(F32)

    def hot(target, the_map):
        step = 128
        for c in range(H // step):
            rows = lax.broadcasted_iota(jnp.int32, (step, H), 0) + c * step
            target[pl.ds(c * step, step), :] = (rows == the_map).astype(F32).astype(BF)

    hot(pr_m, right_map)
    hot(pl_m, left_map)
    ins[5].wait()
    ins[6].wait()
    cinv_p[...] = jnp.zeros_like(cinv_p)
    cinv_p[0:NC, 0:NC] = cv[...]

    def hot_ids(t):
        row = ids_v[pl.ds(t, 1), :]
        rows = lax.broadcasted_iota(jnp.int32, (W, row.shape[1]), 0)
        return (rows == row).astype(F32).astype(BF)

    hot_own = hot_ids(s)
    ins[7].wait()
    mo[r] = dot_nn(hot_own, cmo[r]).astype(BF)

    pl.when(s == S - 1)(send_maps)

    op_copy.wait()
    acc[...] = dot_nt(z0.astype(BF), op_v[:, :H])

    z_copy.wait_recv()
    w_copy.wait_recv()
    w_in = wrecv[...]
    w_hi = w_in.astype(BF)
    w_lo = (w_in - w_hi.astype(F32)).astype(BF)
    pad = lax.broadcasted_iota(jnp.int32, (16, H), 0)
    w_rows = jnp.where(pad == 0, w_hi.astype(F32), jnp.where(pad == 1, w_lo.astype(F32), 0.0))
    gathered = dot_nn(jnp.concatenate([zrecv[...], w_rows.astype(BF)], axis=0), pr_m[...])
    z0_r = gathered[:C]
    w_r = gathered[C : C + 1] + gathered[C + 1 : C + 2]

    col = lax.broadcasted_iota(jnp.int32, (C, W), 1)
    cold = lax.broadcasted_iota(jnp.int32, (C, 128), 1)
    diag = cold == lax.broadcasted_iota(jnp.int32, (C, 128), 0)

    def pick(value, lane):
        return jnp.sum(jnp.where(col == lane, value, 0.0), axis=1, keepdims=True)

    def spread(step, store, ssem, rsem):
        def one(k):
            _, who = peer(k)
            remote(store.at[step, me], store.at[step, me], ssem.at[step, k], rsem.at[step, me], who).start()

        each(G - 1, one)

    def gathered_sum(step, store, ssem, rsem, zero):
        def arrive(k):
            g, who = peer(k)
            remote(store.at[step, g], store.at[step, g], ssem.at[step, 0], rsem.at[step, g], who).wait_recv()

        each(G - 1, arrive)
        if G <= 8:
            total = store[step, 0]
            for g in range(1, G):
                total = total + store[step, g]
            return total
        return lax.fori_loop(0, G, lambda g, t: t + store[step, g], zero)

    def corners(step, z_left, z_right, r_left):
        for q in range(R):
            half = z_left if q < half_r else z_right
            at = (q % half_r) * B
            zs[q] = half[:, at : at + B]
        gamma = jnp.sum(r_left * z_left, axis=1, keepdims=True)
        gamma = jnp.where(r == 0, gamma, 0.0)
        corner = dot_nt(zs[r].astype(BF), mo[r])
        pk[step, me] = corner + jnp.where(col == NC, gamma, 0.0)
        spread(step, pk, pk_ssem, pk_rsem)

    def product(step, local):
        own[step, r] = local.astype(BF)
        delta = jnp.sum(zs[r] * local, axis=1, keepdims=True)
        dk[step, me] = jnp.sum(jnp.where(diag, delta, 0.0), axis=0, keepdims=True)
        spread(step, dk, dk_ssem, dk_rsem)
        mine = own.at[step, r]
        sends = [
            to_side(mine, nbr.at[step], nbr_ssem.at[step], nbr_rsem.at[step], (k + 1) % R) for k in range(R)
        ]
        sends += [
            to_row(mine, own.at[step], own_ssem.at[step], own_rsem.at[step], k) for k in range(1, R)
        ]
        for copy in sends:
            copy.start()
        return sends

    def solve(step):
        total = gathered_sum(step, pk, pk_ssem, pk_rsem, jnp.zeros((C, W), F32))
        solved = lax.dot_general(
            total, cinv_p[...], (((1,), (0,)), ((), ())),
            precision=lax.Precision.HIGHEST, preferred_element_type=F32,
        )
        back = solved.astype(BF)
        gamma = pick(total, NC)
        bend = jnp.sum(total * back.astype(F32), axis=1, keepdims=True)
        return back, gamma, bend

    def joined(store, first, last):
        return jnp.concatenate([store[q] for q in range(first, last)], axis=1)

    def bent(back, first, last):
        return jnp.concatenate(
            [dot_nn(back, mo[q]) + dot_nn(back, mn[q]) for q in range(first, last)], axis=1
        )

    def slope(step, bend):
        total = gathered_sum(step, dk, dk_ssem, dk_rsem, jnp.zeros((1, 128), F32))
        return jnp.sum(jnp.where(diag, total, 0.0), axis=1, keepdims=True) + bend

    def arrive(step):
        for k in range(1, R):
            wait_slot(own.at[step], own_ssem.at[step], own_rsem.at[step], lax.rem(r + k, R))
        for q in range(R):
            wait_slot(nbr.at[step], nbr_ssem.at[step], nbr_rsem.at[step], q)

    corners(0, z0, z0_r, r0)
    pl.when(s != S - 1)(send_maps)
    local0 = acc[...] + dot_nt(z0_r.astype(BF), op_v[:, H:])
    sends0 = product(0, local0)

    for k in range(1, R):
        q = lax.rem(r + k, R)
        wait_slot(cmo, cmo_ssem, cmo_rsem, q)
        mo[q] = dot_nn(hot_own, cmo[q]).astype(BF)
    hot_next = hot_ids(nxt)
    hot_prev = hot_ids(prv)
    for q in range(R):
        wait_slot(cmn, cmn_ssem, cmn_rsem, q)
        mn[q] = dot_nn(hot_next if q < half_r else hot_prev, cmn[q]).astype(BF)
    right = dot_nn(joined(mn, 0, half_r), pr_m[...]).astype(BF)
    left = dot_nn(joined(mn, half_r, R), pl_m[...]).astype(BF)
    for q in range(R):
        at = (q % half_r) * B
        mn[q] = (left if q < half_r else right)[:, at : at + B]

    back0, gamma0, bend0 = solve(0)
    fix_l = bent(back0, 0, half_r)
    fix_r = bent(back0, half_r, R)
    delta0 = slope(0, bend0)
    alpha0 = gamma0 / delta0
    arrive(0)
    wr0 = (joined(own[0], half_r, R).astype(F32) + fix_r + dot_nn(joined(nbr[0], 0, half_r), pr_m[...])) * live_r
    wl0 = (joined(own[0], 0, half_r).astype(F32) + fix_l + dot_nn(joined(nbr[0], half_r, R), pl_m[...])) * live_l
    r1 = r0 - alpha0 * wl0
    z1 = w_l * r1
    z1_r = z0_r - alpha0 * (w_r * wr0)
    corners(1, z1, z1_r, r1)
    local1 = dot_nt(jnp.concatenate([z1.astype(BF), z1_r.astype(BF)], axis=1), op_v[...])
    sends1 = product(1, local1)
    back1, gamma1, bend1 = solve(1)
    fix = bent(back1, 0, half_r)
    beta = gamma1 / gamma0
    delta1 = slope(1, bend1)
    alpha1 = gamma1 / (delta1 - beta * gamma1 / alpha0)
    sol[...] = alpha0 * z0 + alpha1 * (z1 + beta * z0)
    arrive(1)
    wl1 = (joined(own[1], 0, half_r).astype(F32) + fix + dot_nn(joined(nbr[1], half_r, R), pl_m[...])) * live_l
    res[...] = r1 - alpha1 * (wl1 + beta * wl0)

    z_copy.wait_send()
    w_copy.wait_send()
    for copy in cm_sends + sends0 + sends1:
        copy.wait_send()
    for step in range(2):

        def drain(k):
            _, who = peer(k)
            for store, ssem, rsem in ((pk, pk_ssem, pk_rsem), (dk, dk_ssem, dk_rsem)):
                remote(
                    store.at[step, me], store.at[step, me], ssem.at[step, k], rsem.at[step, me], who
                ).wait_send()

        each(G - 1, drain)


def finish(a, b, x, y, sem):
    first = pltpu.make_async_copy(a, x.at[0], sem.at[0])
    second = pltpu.make_async_copy(b, y.at[0], sem.at[1])
    first.start()
    second.start()
    first.wait()
    second.wait()


def per_device(S, R, loads, weights, dual_ops, corner_maps, coarse_inverse, corner_ids,
               iface_sizes, left_partner, right_partner):
    _, C, H = loads.shape
    _, B, full = dual_ops.shape
    J = corner_maps.shape[1]
    NC = coarse_inverse.shape[0]
    W = (NC + 1 + 127) // 128 * 128
    G = S * R
    DMA = pltpu.SemaphoreType.DMA
    hbm = pl.BlockSpec(memory_space=pltpu.HBM)
    vmem = pl.BlockSpec(memory_space=pltpu.VMEM)
    given = [
        pltpu.with_memory_space_constraint(x, pltpu.HBM)
        for x in (loads, weights, dual_ops, corner_maps, coarse_inverse, corner_ids, iface_sizes,
                  left_partner, right_partner)
    ]
    held = pltpu.VMEM((C, H), F32)
    made = pl.pallas_call(
        functools.partial(kernel, S, R),
        out_shape=(held, held),
        in_specs=[hbm] * 9,
        out_specs=(vmem, vmem),
        scratch_shapes=[
            pltpu.VMEM((C, H), F32), pltpu.VMEM((1, H), F32), pltpu.VMEM((B, full), BF),
            pltpu.VMEM((NC, NC), F32), pltpu.VMEM((W, W), F32), pltpu.VMEM(corner_ids.shape, jnp.int32),
            pltpu.VMEM((1, H), jnp.int32), pltpu.VMEM((1, H), jnp.int32), pltpu.SMEM(iface_sizes.shape, jnp.int32),
            pltpu.VMEM((C, H), BF), pltpu.VMEM((C, H), BF), pltpu.VMEM((1, H), F32),
            pltpu.VMEM((R, J, B), BF), pltpu.VMEM((R, J, B), BF),
            pltpu.VMEM((R, W, B), BF), pltpu.VMEM((R, W, B), BF),
            pltpu.VMEM((H, H), BF), pltpu.VMEM((H, H), BF), pltpu.VMEM((R, C, B), F32), pltpu.VMEM((C, B), F32),
            pltpu.VMEM((2, R, C, B), BF), pltpu.VMEM((2, R, C, B), BF), pltpu.VMEM((2, G, C, W), F32),
            pltpu.VMEM((2, G, 1, 128), F32),
            DMA((8,)), DMA, DMA((4,)), DMA((R,)), DMA((R,)), DMA((R,)), DMA((R,)),
            DMA((2, R)), DMA((2, R)), DMA((2, R)), DMA((2, R)), DMA((2, G)), DMA((2, G)), DMA((2, G)), DMA((2, G)),
        ],
        compiler_params=pltpu.CompilerParams(
            collective_id=0, has_side_effects=True, vmem_limit_bytes=LIMIT
        ),
    )(*given)
    done = jax.ShapeDtypeStruct((1, C, H), F32)
    return pl.pallas_call(
        finish,
        out_shape=(done, done),
        in_specs=[vmem] * 2,
        out_specs=(hbm, hbm),
        scratch_shapes=[DMA((2,))],
        compiler_params=pltpu.CompilerParams(vmem_limit_bytes=2**20),
    )(*[pltpu.with_memory_space_constraint(x, pltpu.VMEM) for x in made])


def solution(mesh):
    placed = (
        P(("parts", "sub"), "col", None),
        P(("parts", "sub"), None),
        P(("parts", "sub"), "row", None),
        P(("parts", "sub"), None, "row"),
        P("parts", None),
        P("parts", None),
        P("parts"),
        P(("parts", "sub"), None),
        P(("parts", "sub"), None),
    )
    return jax.shard_map(
        functools.partial(per_device, mesh.shape["sub"], mesh.shape["row"]),
        mesh=mesh,
        in_specs=placed,
        out_specs=(P(("parts", "sub"), "col", None), P(("parts", "sub"), "col", None)),
        check_vma=False,
    )
```

time: 31.3 us -> 25.8 us (0.82)
  local copies, waits for them, and re-layouts: 2.95 us -> 0 us
  Pallas kernels: 27.4 us -> 25 us
    unnamed x2 -> x0, local copies, waits for them, and re-layouts: 2.95 us -> none
    pallas_call x1 -> x2, Pallas kernels: 27.4 us -> 25 us  [the longest x1 24.3 us: per_device(): pl.pallas_call(functools.partial(kernel, S, R), out_shape=(held, held), i...]
where the time goes in v1:
time: 25.8 us; the launch traced here: 25.6 us
  Pallas kernels  25 us (97%)
  between operations  0.64 us (2%)
    pallas_call x1, Pallas kernels, per_device(): pl.pallas_call(functools.partial(kernel, S, R), out_shape=(held, held), i...  24.3 us
    pallas_call x1, Pallas kernels, per_device(): pl.pallas_call(finish, out_shape=(done, done), in_specs=[vmem] * 2, out_s...  0.67 us

profile of v1, /device:TPU:0, one launch (start us, length us, event | category | flops | bytes accessed | tf_op | source)
XLA Modules:
  0.0 25.6 jit_solution(10080495388853274945)
XLA Ops:
  0.6 24.3 %shard_map.104 = (f32[16,1024]{1,0:T(8,128)S(1)}, f32[16,1024]{1,0:T(8,128)S(1)}) custom-call(f32[1,16,1024]{2,1,0:T(8,128)} %loads.1, f32[1,1024]{1,0:T(1,128)} %weights.1, bf16[1,1024,2048]{2,1,0:T(8,128)(2,1)} %op.1, bf16[1,24,1024]{2,1,0:T(8,128)(2,1)} %cm.1, f32[48,48]{1,0:T(8,128)} %cinv.1, s32[4,24]{1,0:T(4,128)} %ids.1, s32[4]{0:T(128)} %sizes.1, ...), custom_call_target="tpu_custom_call" | custom-call | tf_op jit(solution)/shard_map/pallas_call | solution.py:331
  25.0 0.7 %shard_map.105 = (f32[1,16,1024]{2,1,0:T(8,128)}, f32[1,16,1024]{2,1,0:T(8,128)}) custom-call(f32[16,1024]{1,0:T(8,128)S(1)} %get-tuple-element.4.a, f32[16,1024]{1,0:T(8,128)S(1)} %get-tuple-element.5.b), custom_call_target="tpu_custom_call" | custom-call | tf_op jit(solution)/shard_map/pallas_call | solution.py:354

commit v2 on v1

v2 whole, which is shorter than its diff:
```python
import functools

import jax
import jax.numpy as jnp
from jax import lax
from jax.experimental import pallas as pl
from jax.experimental.pallas import tpu as pltpu
from jax.sharding import PartitionSpec as P

MESH = pl.DeviceIdType.MESH
LIMIT = 40 * 2**20
BF = jnp.bfloat16
F32 = jnp.float32


def each(count, body):
    if count <= 8:
        for at in range(count):
            body(at)
    else:
        lax.fori_loop(0, count, lambda at, _: (body(at), 0)[1], 0)


def dot_nt(a, b):
    return lax.dot_general(a, b, (((1,), (1,)), ((), ())), preferred_element_type=F32)


def dot_nn(a, b):
    return lax.dot_general(a, b, (((1,), (0,)), ((), ())), preferred_element_type=F32)


def kernel(
    S, R, loads, weights, op, cm, cinv, ids, sizes, lmap, rmap, sol, res,
    loads_v, w_v, op_v, cv, cinv_p, ids_v, lmap_v, rmap_v, sizes_v,
    zsend, zrecv, wrecv, cm_v, cmo, cmn, mm, hots, zs, acc, turned, zz, wt, live, fixed, met, sol_v, res_v,
    blocks, pk, dk,
    in_sem, op_sem, z_sem, cmo_ssem, cmo_rsem, cmn_ssem, cmn_rsem,
    blk_ssem, own_rsem, nbr_rsem, pk_ssem, pk_rsem, dk_ssem, dk_rsem, out_sem,
):
    s = lax.axis_index("sub")
    r = lax.axis_index("row")
    G = S * R
    me = s * R + r
    C, H = loads_v.shape
    B = op_v.shape[0]
    NC = cv.shape[0]
    W = cinv_p.shape[0]
    half_r = R // 2
    nxt = lax.rem(s + 1, S)
    prv = lax.rem(s + S - 1, S)
    side = r // half_r
    toward = lax.rem(s + S - 1 + 2 * side, S)

    barrier = pltpu.get_barrier_semaphore()

    def peer(k):
        g = lax.rem(me + k + 1, G)
        return g, {"sub": g // R, "row": lax.rem(g, R)}

    def greet(k):
        _, who = peer(k)
        pl.semaphore_signal(barrier, inc=1, device_id=who, device_id_type=MESH)

    each(G - 1, greet)

    ins = [
        pltpu.make_async_copy(src, dst, in_sem.at[i])
        for i, (src, dst) in enumerate([
            (loads.at[0], loads_v), (weights, w_v), (sizes, sizes_v), (rmap, rmap_v), (lmap, lmap_v),
            (ids, ids_v), (cinv, cv), (cm.at[0], cm_v),
        ])
    ]
    for copy in ins:
        copy.start()
    op_copy = pltpu.make_async_copy(op.at[0], op_v, op_sem)
    op_copy.start()

    for copy in ins[:3]:
        copy.wait()
    lanes = lax.broadcasted_iota(jnp.int32, (1, H), 1)
    live_l = (lanes < sizes_v[prv]).astype(F32)
    live[0] = live_l
    size_after = sizes_v[s]
    w_l = w_v[...]
    r0 = loads_v[...] * live_l
    z0 = w_l * r0
    zsend[...] = z0.astype(BF)
    zz[0] = z0
    wt[0] = w_l

    ins[7].wait()
    J = cm_v.shape[0]
    J0 = cmo.shape[1]
    own_map = cm_v[...].astype(F32)
    if J0 < J:
        tail = own_map[J0:]
        folded = jnp.concatenate([tail[:, : B // 2], tail[:, B // 2 :]], axis=0)
        cmo[r] = jnp.concatenate([own_map[:J0], folded], axis=1).astype(BF)
    else:
        cmo[r] = own_map.astype(BF)

    def spreadout(hot, kept):
        if J0 == J:
            return dot_nn(hot, kept)
        tail = kept[:, B:].astype(F32)
        lower = jnp.concatenate([tail[: J - J0], tail[J - J0 :]], axis=1)
        return dot_nn(hot, jnp.concatenate([kept[:, :B].astype(F32), lower], axis=0).astype(BF))

    pl.semaphore_wait(barrier, G - 1)

    def remote(src, dst, ssem, rsem, who):
        return pltpu.make_async_remote_copy(
            src_ref=src, dst_ref=dst, send_sem=ssem, recv_sem=rsem, device_id=who, device_id_type=MESH
        )

    z_copy = remote(zsend, zrecv, z_sem.at[0], z_sem.at[1], {"sub": prv})
    w_copy = remote(w_v, wrecv, z_sem.at[2], z_sem.at[3], {"sub": prv})
    z_copy.start()
    w_copy.start()

    def to_row(src, dst, ssem, rsem, k):
        return remote(src, dst.at[r], ssem, rsem, {"row": lax.rem(r + k, R)})

    def to_side(src, dst, ssem, rsem, k):
        return remote(src, dst.at[r], ssem, rsem, {"sub": toward, "row": lax.rem(r + k, R)})

    def wait_slot(dst, rsem, q):
        remote(dst.at[q], dst.at[q], rsem, rsem, {"sub": nxt}).wait_recv()

    cm_sides = [to_side(cmo.at[r], cmn, cmn_ssem.at[k], cmn_rsem.at[k], k) for k in range(R)]
    cm_rows = [to_row(cmo.at[r], cmo, cmo_ssem.at[k - 1], cmo_rsem.at[k - 1], k) for k in range(1, R)]
    for copy in cm_rows + cm_sides[:1]:
        copy.start()

    ins[3].wait()
    ins[4].wait()
    right_map = rmap_v[...]
    left_map = lmap_v[...]
    live[1] = (right_map < size_after).astype(F32)

    def hot(target, the_map):
        step = 128
        for c in range(H // step):
            rows = lax.broadcasted_iota(jnp.int32, (step, H), 0) + c * step
            target[pl.ds(c * step, step), :] = (rows == the_map).astype(F32).astype(BF)

    hot(hots.at[1], right_map)
    hot(hots.at[0], left_map)
    ins[5].wait()
    ins[6].wait()
    cinv_p[...] = jnp.zeros_like(cinv_p)
    cinv_p[0:NC, 0:NC] = cv[...]

    def hot_ids(t):
        row = ids_v[pl.ds(t, 1), :]
        rows = lax.broadcasted_iota(jnp.int32, (W, row.shape[1]), 0)
        return (rows == row).astype(F32).astype(BF)

    hot_own = hot_ids(s)
    mm[r, 0:W] = spreadout(hot_own, cmo[r]).astype(BF)

    op_copy.wait()
    step = 256
    for c in range(2 * H // step):
        turned[c * step // H, c * step % H : c * step % H + step, :] = op_v[:, c * step : (c + 1) * step].T
    acc[...] = dot_nn(z0.astype(BF), turned[0])

    for copy in cm_sides[1:]:
        copy.start()
    z_copy.wait_recv()
    w_copy.wait_recv()
    w_in = wrecv[...]
    w_hi = w_in.astype(BF)
    w_lo = (w_in - w_hi.astype(F32)).astype(BF)
    pad = lax.broadcasted_iota(jnp.int32, (16, H), 0)
    w_rows = jnp.where(pad == 0, w_hi.astype(F32), jnp.where(pad == 1, w_lo.astype(F32), 0.0))
    gathered = dot_nn(jnp.concatenate([zrecv[...], w_rows.astype(BF)], axis=0), hots[1])
    z0_r = gathered[:C]
    zz[1] = z0_r
    wt[1] = gathered[C : C + 1] + gathered[C + 1 : C + 2]

    col = lax.broadcasted_iota(jnp.int32, (C, W), 1)
    cold = lax.broadcasted_iota(jnp.int32, (C, 128), 1)
    diag = cold == lax.broadcasted_iota(jnp.int32, (C, 128), 0)

    def pick(value, lane):
        return jnp.sum(jnp.where(col == lane, value, 0.0), axis=1, keepdims=True)

    fold = C == 16 and W == 128 and NC < 64

    def packed(value):
        return value[:8] + pltpu.roll(value[8:], 64, 1) if fold else value

    def unpacked(value):
        if not fold:
            return value
        low = lax.broadcasted_iota(jnp.int32, value.shape, 1) < 64
        return jnp.concatenate(
            [jnp.where(low, value, 0.0), pltpu.roll(jnp.where(low, 0.0, value), 64, 1)], axis=0
        )

    def spread(step, store, ssem, rsem):
        def one(k):
            _, who = peer(k)
            remote(store.at[step, me], store.at[step, me], ssem.at[step], rsem.at[step], who).start()

        each(G - 1, one)

    def gathered_sum(step, store, ssem, rsem, zero):
        rest = store.at[step, pl.ds(0, G - 1)]
        remote(rest, rest, ssem.at[step], rsem.at[step], {"sub": nxt}).wait_recv()
        if G <= 8:
            total = store[step, 0]
            for g in range(1, G):
                total = total + store[step, g]
            return total
        return lax.fori_loop(0, G, lambda g, t: t + store[step, g], zero)

    def split(d, z):
        for j in range(half_r):
            zs[d * half_r + j] = z[:, j * B : (j + 1) * B]

    def corners(step, r_left, z_left):
        gamma = jnp.sum(r_left * z_left, axis=1, keepdims=True)
        gamma = jnp.where(r == 0, gamma, 0.0)
        corner = dot_nt(zs[r].astype(BF), mm[r, 0:W])
        pk[step, me] = packed(corner + jnp.where(col == NC, gamma, 0.0))
        spread(step, pk, pk_ssem, pk_rsem)

    def product(step, local):
        blocks[step, r] = local.astype(BF)
        mine = blocks.at[step, r]
        delta = jnp.sum(zs[r] * local, axis=1, keepdims=True)
        dk[step, me] = jnp.sum(jnp.where(diag, delta, 0.0), axis=0, keepdims=True)
        spread(step, dk, dk_ssem, dk_rsem)
        nbr = blocks.at[step, pl.ds(R, R)]
        sides = [to_side(mine, nbr, blk_ssem.at[step], nbr_rsem.at[step, k], k) for k in range(R)]
        rows = [to_row(mine, blocks.at[step], blk_ssem.at[step], own_rsem.at[step, k - 1], k) for k in range(1, R)]

        def start(copies):
            for copy in copies:
                copy.start()

        if step == 0:
            start(rows + sides)
        else:
            pl.when(side == 0)(lambda: start(rows))
            pl.when(side == 1)(lambda: start(sides[1:] + sides[:1]))

    def solve(step):
        total = unpacked(gathered_sum(step, pk, pk_ssem, pk_rsem, jnp.zeros(pk.shape[2:], F32)))
        solved = lax.dot_general(
            total, cinv_p[...], (((1,), (0,)), ((), ())),
            precision=lax.Precision.HIGHEST, preferred_element_type=F32,
        )
        back = solved.astype(BF)
        gamma = pick(total, NC)
        bend = jnp.sum(total * back.astype(F32), axis=1, keepdims=True)
        return back, gamma, bend

    def bent(back, first, last):
        twice = jnp.concatenate([back, back], axis=1)
        return jnp.concatenate([dot_nn(twice, mm[q]) for q in range(first, last)], axis=1)

    def slope(step, total, bend):
        return jnp.sum(jnp.where(diag, total, 0.0), axis=1, keepdims=True) + bend

    def meet_own(step):
        for k in range(1, R):
            q = lax.rem(r + R - k, R)
            take = functools.partial(wait_slot, blocks.at[step], own_rsem.at[step, k - 1], q)
            if step == 0:
                take()
            else:
                pl.when(q < half_r)(take)

    def meet(step, d):
        for j in range(half_r):
            q = (1 - d) * half_r + j
            wait_slot(blocks.at[step], nbr_rsem.at[step, lax.rem(r - q + R, R)], R + q)

    def meeting(step, d):
        start = (1 - d) * half_r
        theirs = jnp.concatenate([blocks[step, R + start + j] for j in range(half_r)], axis=1)
        mine = jnp.concatenate([blocks[step, d * half_r + j] for j in range(half_r)], axis=1)
        return mine.astype(F32) + dot_nn(theirs, hots[d])

    split(0, z0)
    split(1, z0_r)
    corners(0, r0, z0)
    local0 = acc[...] + dot_nn(z0_r.astype(BF), turned[1])
    product(0, local0)

    for k in range(1, R):
        q = lax.rem(r + R - k, R)
        wait_slot(cmo, cmo_rsem.at[k - 1], q)
        mm[q, 0:W] = spreadout(hot_own, cmo[q]).astype(BF)
    hot_next = hot_ids(nxt)
    hot_prev = hot_ids(prv)
    for k in range(R):
        wait_slot(cmn, cmn_rsem.at[k], lax.rem(r + R - k, R))
    for q in range(R):
        mm[q, W : 2 * W] = spreadout(hot_next if q < half_r else hot_prev, cmn[q]).astype(BF)
    right = dot_nn(jnp.concatenate([mm[q, W : 2 * W] for q in range(half_r)], axis=1), hots[1]).astype(BF)
    left = dot_nn(jnp.concatenate([mm[q, W : 2 * W] for q in range(half_r, R)], axis=1), hots[0]).astype(BF)
    for q in range(R):
        at = (q % half_r) * B
        mm[q, W : 2 * W] = (left if q < half_r else right)[:, at : at + B]

    early = jnp.where(s == 0, 1, 0)
    late = 1 - early
    meet_own(0)
    meet(0, early)
    met[early] = meeting(0, early)
    back0, gamma0, bend0 = solve(0)
    fixed[0] = bent(back0, 0, half_r)
    fixed[1] = bent(back0, half_r, R)
    steep0 = gathered_sum(0, dk, dk_ssem, dk_rsem, jnp.zeros((1, 128), F32))
    meet(0, late)
    delta0 = slope(0, steep0, bend0)
    alpha0 = gamma0 / delta0

    def advance(d):
        met[d] = (met[d] + fixed[d]) * live[d]
        z = zz[d] - alpha0 * (wt[d] * met[d])
        split(d, z)
        return z.astype(BF)

    met[late] = meeting(0, late)
    acc[...] = dot_nn(advance(early), turned[early])
    last = advance(late)
    wl0 = met[0]
    r1 = r0 - alpha0 * wl0
    z1 = jnp.concatenate([zs[q] for q in range(half_r)], axis=1)
    corners(1, r1, z1)
    local1 = acc[...] + dot_nn(last, turned[late])
    product(1, local1)
    back1, gamma1, bend1 = solve(1)
    fix = bent(back1, 0, half_r)
    beta = gamma1 / gamma0
    steep1 = gathered_sum(1, dk, dk_ssem, dk_rsem, jnp.zeros((1, 128), F32))
    meet_own(1)
    meet(1, 0)
    delta1 = slope(1, steep1, bend1)
    alpha1 = gamma1 / (delta1 - beta * gamma1 / alpha0)
    sol_v[...] = alpha0 * z0 + alpha1 * (z1 + beta * z0)
    sol_out = pltpu.make_async_copy(sol_v, sol, out_sem.at[0])
    sol_out.start()
    wl1 = (meeting(1, 0) + fix) * live[0]
    res_v[...] = r1 - alpha1 * (wl1 + beta * wl0)
    res_out = pltpu.make_async_copy(res_v, res, out_sem.at[1])
    res_out.start()

    z_copy.wait_send()
    w_copy.wait_send()
    for copy in cm_sides + cm_rows:
        copy.wait_send()
    for step in range(2):
        def sent(count):
            gone = blocks.at[step, pl.ds(0, count)]
            remote(gone, gone, blk_ssem.at[step], blk_ssem.at[step], {"sub": nxt}).wait_send()

        if step == 0:
            sent(2 * R - 1)
        else:
            pl.when(side == 0)(functools.partial(sent, R - 1))
            pl.when(side == 1)(functools.partial(sent, R))
        for store, ssem, rsem in ((pk, pk_ssem, pk_rsem), (dk, dk_ssem, dk_rsem)):
            rest = store.at[step, pl.ds(0, G - 1)]
            remote(rest, rest, ssem.at[step], rsem.at[step], {"sub": nxt}).wait_send()
    sol_out.wait()
    res_out.wait()


def finish(a, b, x, y, sem):
    first = pltpu.make_async_copy(a, x.at[0], sem.at[0])
    second = pltpu.make_async_copy(b, y.at[0], sem.at[1])
    first.start()
    second.start()
    first.wait()
    second.wait()


def per_device(S, R, loads, weights, dual_ops, corner_maps, coarse_inverse, corner_ids,
               iface_sizes, left_partner, right_partner):
    _, C, H = loads.shape
    _, B, full = dual_ops.shape
    J = corner_maps.shape[1]
    NC = coarse_inverse.shape[0]
    W = (NC + 1 + 127) // 128 * 128
    G = S * R
    fold = (16 * (J // 16), B + B // 2) if J % 16 == 8 and J < 32 else (J, B)
    DMA = pltpu.SemaphoreType.DMA
    hbm = pl.BlockSpec(memory_space=pltpu.HBM)
    vmem = pl.BlockSpec(memory_space=pltpu.VMEM)
    given = [
        pltpu.with_memory_space_constraint(x, pltpu.HBM)
        for x in (loads, weights, dual_ops, corner_maps, coarse_inverse, corner_ids, iface_sizes,
                  left_partner, right_partner)
    ]
    held = pltpu.VMEM((C, H), F32)
    made = pl.pallas_call(
        functools.partial(kernel, S, R),
        out_shape=(held, held),
        in_specs=[hbm] * 9,
        out_specs=(pl.BlockSpec(memory_space=pl.ANY),) * 2,
        scratch_shapes=[
            pltpu.VMEM((C, H), F32), pltpu.VMEM((1, H), F32), pltpu.VMEM((B, full), BF),
            pltpu.VMEM((NC, NC), F32), pltpu.VMEM((W, W), F32), pltpu.VMEM(corner_ids.shape, jnp.int32),
            pltpu.VMEM((1, H), jnp.int32), pltpu.VMEM((1, H), jnp.int32), pltpu.SMEM(iface_sizes.shape, jnp.int32),
            pltpu.VMEM((C, H), BF), pltpu.VMEM((C, H), BF), pltpu.VMEM((1, H), F32),
            pltpu.VMEM((J, B), BF), pltpu.VMEM((R,) + fold, BF), pltpu.VMEM((R,) + fold, BF),
            pltpu.VMEM((R, 2 * W, B), BF),
            pltpu.VMEM((2, H, H), BF), pltpu.VMEM((R, C, B), F32), pltpu.VMEM((C, B), F32),
            pltpu.VMEM((2, H, B), BF), pltpu.VMEM((2, C, H), F32), pltpu.VMEM((2, 1, H), F32), pltpu.VMEM((2, 1, H), F32),
            pltpu.VMEM((2, C, H), F32), pltpu.VMEM((2, C, H), F32), pltpu.VMEM((C, H), F32), pltpu.VMEM((C, H), F32),
            pltpu.VMEM((2, 2 * R, C, B), BF), pltpu.VMEM((2, G, 8 if C == 16 and W == 128 and NC < 64 else C, W), F32),
            pltpu.VMEM((2, G, 1, 128), F32),
            DMA((8,)), DMA, DMA((4,)), DMA((R - 1,)), DMA((R - 1,)), DMA((R,)), DMA((R,)),
            DMA((2,)), DMA((2, R - 1)), DMA((2, R)), DMA((2,)), DMA((2,)), DMA((2,)), DMA((2,)), DMA((2,)),
        ],
        compiler_params=pltpu.CompilerParams(
            collective_id=0, has_side_effects=True, vmem_limit_bytes=LIMIT
        ),
    )(*given)
    done = jax.ShapeDtypeStruct((1, C, H), F32)
    return pl.pallas_call(
        finish,
        out_shape=(done, done),
        in_specs=[vmem] * 2,
        out_specs=(hbm, hbm),
        scratch_shapes=[DMA((2,))],
        compiler_params=pltpu.CompilerParams(vmem_limit_bytes=2**20),
    )(*[pltpu.with_memory_space_constraint(x, pltpu.VMEM) for x in made])


def solution(mesh):
    placed = (
        P(("parts", "sub"), "col", None),
        P(("parts", "sub"), None),
        P(("parts", "sub"), "row", None),
        P(("parts", "sub"), None, "row"),
        P("parts", None),
        P("parts", None),
        P("parts"),
        P(("parts", "sub"), None),
        P(("parts", "sub"), None),
    )
    return jax.shard_map(
        functools.partial(per_device, mesh.shape["sub"], mesh.shape["row"]),
        mesh=mesh,
        in_specs=placed,
        out_specs=(P(("parts", "sub"), "col", None), P(("parts", "sub"), "col", None)),
        check_vma=False,
    )
```

time: 25.8 us -> 23.3 us (0.903)
  Pallas kernels: 25 us -> 22.5 us
    pallas_call x1, Pallas kernels: 24.3 us -> 21.8 us  [per_device(): pl.pallas_call(functools.partial(kernel, S, R), out_shape=(held, held), i...]
where the time goes in v2:
time: 23.3 us; the launch traced here: 23.1 us
  Pallas kernels  22.5 us (97%)
  between operations  0.64 us (3%)
    pallas_call x1, Pallas kernels, per_device(): pl.pallas_call(functools.partial(kernel, S, R), out_shape=(held, held), i...  21.8 us
    pallas_call x1, Pallas kernels, per_device(): pl.pallas_call(finish, out_shape=(done, done), in_specs=[vmem] * 2, out_s...  0.67 us

profile of v2, /device:TPU:0, one launch (start us, length us, event | category | flops | bytes accessed | tf_op | source)
XLA Modules:
  0.0 23.1 jit_solution(5385396996235618381)
XLA Ops:
  0.6 21.8 %shard_map.104 = (f32[16,1024]{1,0:T(8,128)S(1)}, f32[16,1024]{1,0:T(8,128)S(1)}) custom-call(f32[1,16,1024]{2,1,0:T(8,128)} %loads.1, f32[1,1024]{1,0:T(1,128)} %weights.1, bf16[1,1024,2048]{2,1,0:T(8,128)(2,1)} %op.1, bf16[1,24,1024]{2,1,0:T(8,128)(2,1)} %cm.1, f32[48,48]{1,0:T(8,128)} %cinv.1, s32[4,24]{1,0:T(4,128)} %ids.1, s32[4]{0:T(128)} %sizes.1, ...), custom_call_target="tpu_custom_call" | custom-call | tf_op jit(solution)/shard_map/pallas_call | solution.py:402
  22.5 0.7 %shard_map.105 = (f32[1,16,1024]{2,1,0:T(8,128)}, f32[1,16,1024]{2,1,0:T(8,128)}) custom-call(f32[16,1024]{1,0:T(8,128)S(1)} %get-tuple-element.4.a, f32[16,1024]{1,0:T(8,128)S(1)} %get-tuple-element.5.b), custom_call_target="tpu_custom_call" | custom-call | tf_op jit(solution)/shard_map/pallas_call | solution.py:427

commit v3 on v2

--- a/solution.py
+++ b/solution.py
@@ -32,10 +32,10 @@
 def kernel(
     S, R, loads, weights, op, cm, cinv, ids, sizes, lmap, rmap, sol, res,
     loads_v, w_v, op_v, cv, cinv_p, ids_v, lmap_v, rmap_v, sizes_v,
-    zsend, zrecv, wrecv, cm_v, cmo, cmn, mm, hots, zs, acc, turned, zz, wt, live, fixed, met, sol_v, res_v,
+    zsend, zrecv, wrecv, cm_v, cmo, cmn, mm, hots, zs, acc, turned, zz, wt, live, fixed, met,
     blocks, pk, dk,
     in_sem, op_sem, z_sem, cmo_ssem, cmo_rsem, cmn_ssem, cmn_rsem,
-    blk_ssem, own_rsem, nbr_rsem, pk_ssem, pk_rsem, dk_ssem, dk_rsem, out_sem,
+    blk_ssem, own_rsem, nbr_rsem, pk_ssem, pk_rsem, dk_ssem, dk_rsem, ready,
 ):
     s = lax.axis_index("sub")
     r = lax.axis_index("row")
@@ -61,7 +61,21 @@
         _, who = peer(k)
         pl.semaphore_signal(barrier, inc=1, device_id=who, device_id_type=MESH)
 
-    each(G - 1, greet)
+    def tell(semaphore, k):
+        pl.semaphore_signal(
+            semaphore, inc=1, device_id={"row": lax.rem(r + k, R)}, device_id_type=MESH
+        )
+
+    close = S <= 4
+    if close:
+        for other in (nxt, prv) if S > 2 else (nxt,):
+            pl.semaphore_signal(barrier, inc=1, device_id={"sub": other}, device_id_type=MESH)
+        for k in range(1, R):
+            tell(barrier, k)
+        met_first = (2 if S > 2 else 1) + R - 1
+    else:
+        each(G - 1, greet)
+        met_first = G - 1
 
     ins = [
         pltpu.make_async_copy(src, dst, in_sem.at[i])
@@ -106,7 +120,7 @@
         lower = jnp.concatenate([tail[: J - J0], tail[J - J0 :]], axis=1)
         return dot_nn(hot, jnp.concatenate([kept[:, :B].astype(F32), lower], axis=0).astype(BF))
 
-    pl.semaphore_wait(barrier, G - 1)
+    pl.semaphore_wait(barrier, met_first)
 
     def remote(src, dst, ssem, rsem, who):
         return pltpu.make_async_remote_copy(
@@ -117,6 +131,8 @@
     w_copy = remote(w_v, wrecv, z_sem.at[2], z_sem.at[3], {"sub": prv})
     z_copy.start()
     w_copy.start()
+    for k in range(1, R):
+        tell(ready.at[0], k)
 
     def to_row(src, dst, ssem, rsem, k):
         return remote(src, dst.at[r], ssem, rsem, {"row": lax.rem(r + k, R)})
@@ -129,8 +145,13 @@
 
     cm_sides = [to_side(cmo.at[r], cmn, cmn_ssem.at[k], cmn_rsem.at[k], k) for k in range(R)]
     cm_rows = [to_row(cmo.at[r], cmo, cmo_ssem.at[k - 1], cmo_rsem.at[k - 1], k) for k in range(1, R)]
-    for copy in cm_rows + cm_sides[:1]:
-        copy.start()
+    def launch(copies):
+        for copy in copies:
+            copy.start()
+
+    far = jnp.logical_or(s == 0, s == S - 1)
+    launch(cm_sides[:1])
+    launch(cm_rows)
 
     ins[3].wait()
     ins[4].wait()
@@ -151,6 +172,9 @@
     cinv_p[...] = jnp.zeros_like(cinv_p)
     cinv_p[0:NC, 0:NC] = cv[...]
 
+    pl.semaphore_wait(ready.at[0], R - 1)
+    pl.when(far)(lambda: launch(cm_sides[1:]))
+
     def hot_ids(t):
         row = ids_v[pl.ds(t, 1), :]
         rows = lax.broadcasted_iota(jnp.int32, (W, row.shape[1]), 0)
@@ -165,10 +189,15 @@
         turned[c * step // H, c * step % H : c * step % H + step, :] = op_v[:, c * step : (c + 1) * step].T
     acc[...] = dot_nn(z0.astype(BF), turned[0])
 
-    for copy in cm_sides[1:]:
-        copy.start()
+    for k in range(1, R):
+        q = lax.rem(r + R - k, R)
+        wait_slot(cmo, cmo_rsem.at[k - 1], q)
+        mm[q, 0:W] = spreadout(hot_own, cmo[q]).astype(BF)
+    pl.when(jnp.logical_not(far))(lambda: launch(cm_sides[1:]))
     z_copy.wait_recv()
     w_copy.wait_recv()
+    for k in range(1, R):
+        tell(ready.at[1], k)
     w_in = wrecv[...]
     w_hi = w_in.astype(BF)
     w_lo = (w_in - w_hi.astype(F32)).astype(BF)
@@ -200,52 +229,56 @@
         )
 
     def spread(step, store, ssem, rsem):
+        count = store.shape[1]
+        slot = me if count == G else s
+
         def one(k):
-            _, who = peer(k)
-            remote(store.at[step, me], store.at[step, me], ssem.at[step], rsem.at[step], who).start()
-
-        each(G - 1, one)
+            who = peer(k)[1] if count == G else {"sub": lax.rem(s + k + 1, S)}
+            remote(store.at[step, slot], store.at[step, slot], ssem.at[step], rsem.at[step], who).start()
+
+        each(count - 1, one)
 
     def gathered_sum(step, store, ssem, rsem, zero):
-        rest = store.at[step, pl.ds(0, G - 1)]
+        count = store.shape[1]
+        rest = store.at[step, pl.ds(0, count - 1)]
         remote(rest, rest, ssem.at[step], rsem.at[step], {"sub": nxt}).wait_recv()
-        if G <= 8:
+        if count <= 8:
             total = store[step, 0]
-            for g in range(1, G):
+            for g in range(1, count):
                 total = total + store[step, g]
             return total
-        return lax.fori_loop(0, G, lambda g, t: t + store[step, g], zero)
+        return lax.fori_loop(0, count, lambda g, t: t + store[step, g], zero)
 
     def split(d, z):
         for j in range(half_r):
             zs[d * half_r + j] = z[:, j * B : (j + 1) * B]
 
-    def corners(step, r_left, z_left):
-        gamma = jnp.sum(r_left * z_left, axis=1, keepdims=True)
-        gamma = jnp.where(r == 0, gamma, 0.0)
-        corner = dot_nt(zs[r].astype(BF), mm[r, 0:W])
-        pk[step, me] = packed(corner + jnp.where(col == NC, gamma, 0.0))
-        spread(step, pk, pk_ssem, pk_rsem)
-
-    def product(step, local):
+    def product(step, local, r_left, z_left):
         blocks[step, r] = local.astype(BF)
         mine = blocks.at[step, r]
         delta = jnp.sum(zs[r] * local, axis=1, keepdims=True)
         dk[step, me] = jnp.sum(jnp.where(diag, delta, 0.0), axis=0, keepdims=True)
-        spread(step, dk, dk_ssem, dk_rsem)
+        gamma = jnp.sum(r_left * z_left, axis=1, keepdims=True)
+        corner = jnp.where(col == NC, gamma, 0.0)
+        for q in range(R):
+            corner = corner + dot_nt(zs[q].astype(BF), mm[q, 0:W])
+        pk[step, s] = packed(corner)
         nbr = blocks.at[step, pl.ds(R, R)]
         sides = [to_side(mine, nbr, blk_ssem.at[step], nbr_rsem.at[step, k], k) for k in range(R)]
         rows = [to_row(mine, blocks.at[step], blk_ssem.at[step], own_rsem.at[step, k - 1], k) for k in range(1, R)]
 
-        def start(copies):
-            for copy in copies:
-                copy.start()
-
+        spread(step, pk, pk_ssem, pk_rsem)
         if step == 0:
-            start(rows + sides)
+            launch(rows)
         else:
-            pl.when(side == 0)(lambda: start(rows))
-            pl.when(side == 1)(lambda: start(sides[1:] + sides[:1]))
+            pl.when(side == 0)(lambda: launch(rows))
+        if step == 0:
+            pl.semaphore_wait(ready.at[1], R - 1)
+        spread(step, dk, dk_ssem, dk_rsem)
+        if step == 0:
+            launch(sides)
+        else:
+            pl.when(side == 1)(lambda: launch(sides[1:] + sides[:1]))
 
     def solve(step):
         total = unpacked(gathered_sum(step, pk, pk_ssem, pk_rsem, jnp.zeros(pk.shape[2:], F32)))
@@ -287,14 +320,9 @@
 
     split(0, z0)
     split(1, z0_r)
-    corners(0, r0, z0)
     local0 = acc[...] + dot_nn(z0_r.astype(BF), turned[1])
-    product(0, local0)
-
-    for k in range(1, R):
-        q = lax.rem(r + R - k, R)
-        wait_slot(cmo, cmo_rsem.at[k - 1], q)
-        mm[q, 0:W] = spreadout(hot_own, cmo[q]).astype(BF)
+    product(0, local0, r0, z0)
+
     hot_next = hot_ids(nxt)
     hot_prev = hot_ids(prv)
     for k in range(R):
@@ -316,7 +344,6 @@
     fixed[0] = bent(back0, 0, half_r)
     fixed[1] = bent(back0, half_r, R)
     steep0 = gathered_sum(0, dk, dk_ssem, dk_rsem, jnp.zeros((1, 128), F32))
-    meet(0, late)
     delta0 = slope(0, steep0, bend0)
     alpha0 = gamma0 / delta0
 
@@ -326,30 +353,26 @@
         split(d, z)
         return z.astype(BF)
 
+    acc[...] = dot_nn(advance(early), turned[early])
+    meet(0, late)
     met[late] = meeting(0, late)
-    acc[...] = dot_nn(advance(early), turned[early])
     last = advance(late)
     wl0 = met[0]
     r1 = r0 - alpha0 * wl0
     z1 = jnp.concatenate([zs[q] for q in range(half_r)], axis=1)
-    corners(1, r1, z1)
     local1 = acc[...] + dot_nn(last, turned[late])
-    product(1, local1)
+    product(1, local1, r1, z1)
     back1, gamma1, bend1 = solve(1)
     fix = bent(back1, 0, half_r)
     beta = gamma1 / gamma0
     steep1 = gathered_sum(1, dk, dk_ssem, dk_rsem, jnp.zeros((1, 128), F32))
+    delta1 = slope(1, steep1, bend1)
+    alpha1 = gamma1 / (delta1 - beta * gamma1 / alpha0)
+    sol[...] = alpha0 * z0 + alpha1 * (z1 + beta * z0)
+    part = r1 - (alpha1 * beta) * wl0
     meet_own(1)
     meet(1, 0)
-    delta1 = slope(1, steep1, bend1)
-    alpha1 = gamma1 / (delta1 - beta * gamma1 / alpha0)
-    sol_v[...] = alpha0 * z0 + alpha1 * (z1 + beta * z0)
-    sol_out = pltpu.make_async_copy(sol_v, sol, out_sem.at[0])
-    sol_out.start()
-    wl1 = (meeting(1, 0) + fix) * live[0]
-    res_v[...] = r1 - alpha1 * (wl1 + beta * wl0)
-    res_out = pltpu.make_async_copy(res_v, res, out_sem.at[1])
-    res_out.start()
+    res[...] = part - alpha1 * ((meeting(1, 0) + fix) * live[0])
 
     z_copy.wait_send()
     w_copy.wait_send()
@@ -366,10 +389,8 @@
             pl.when(side == 0)(functools.partial(sent, R - 1))
             pl.when(side == 1)(functools.partial(sent, R))
         for store, ssem, rsem in ((pk, pk_ssem, pk_rsem), (dk, dk_ssem, dk_rsem)):
-            rest = store.at[step, pl.ds(0, G - 1)]
+            rest = store.at[step, pl.ds(0, store.shape[1] - 1)]
             remote(rest, rest, ssem.at[step], rsem.at[step], {"sub": nxt}).wait_send()
-    sol_out.wait()
-    res_out.wait()
 
 
 def finish(a, b, x, y, sem):
@@ -403,7 +424,7 @@
         functools.partial(kernel, S, R),
         out_shape=(held, held),
         in_specs=[hbm] * 9,
-        out_specs=(pl.BlockSpec(memory_space=pl.ANY),) * 2,
+        out_specs=(vmem, vmem),
         scratch_shapes=[
             pltpu.VMEM((C, H), F32), pltpu.VMEM((1, H), F32), pltpu.VMEM((B, full), BF),
             pltpu.VMEM((NC, NC), F32), pltpu.VMEM((W, W), F32), pltpu.VMEM(corner_ids.shape, jnp.int32),
@@ -413,11 +434,11 @@
             pltpu.VMEM((R, 2 * W, B), BF),
             pltpu.VMEM((2, H, H), BF), pltpu.VMEM((R, C, B), F32), pltpu.VMEM((C, B), F32),
             pltpu.VMEM((2, H, B), BF), pltpu.VMEM((2, C, H), F32), pltpu.VMEM((2, 1, H), F32), pltpu.VMEM((2, 1, H), F32),
-            pltpu.VMEM((2, C, H), F32), pltpu.VMEM((2, C, H), F32), pltpu.VMEM((C, H), F32), pltpu.VMEM((C, H), F32),
-            pltpu.VMEM((2, 2 * R, C, B), BF), pltpu.VMEM((2, G, 8 if C == 16 and W == 128 and NC < 64 else C, W), F32),
+            pltpu.VMEM((2, C, H), F32), pltpu.VMEM((2, C, H), F32),
+            pltpu.VMEM((2, 2 * R, C, B), BF), pltpu.VMEM((2, S, 8 if C == 16 and W == 128 and NC < 64 else C, W), F32),
             pltpu.VMEM((2, G, 1, 128), F32),
             DMA((8,)), DMA, DMA((4,)), DMA((R - 1,)), DMA((R - 1,)), DMA((R,)), DMA((R,)),
-            DMA((2,)), DMA((2, R - 1)), DMA((2, R)), DMA((2,)), DMA((2,)), DMA((2,)), DMA((2,)), DMA((2,)),
+            DMA((2,)), DMA((2, R - 1)), DMA((2, R)), DMA((2,)), DMA((2,)), DMA((2,)), DMA((2,)), pltpu.SemaphoreType.REGULAR((2,)),
         ],
         compiler_params=pltpu.CompilerParams(
             collective_id=0, has_side_effects=True, vmem_limit_bytes=LIMIT

time: 23.3 us -> 22.3 us (0.957)
  Pallas kernels: 22.5 us -> 21.5 us
    pallas_call x1, Pallas kernels: 21.8 us -> 20.8 us  [per_device(): pl.pallas_call(functools.partial(kernel, S, R), out_shape=(held, held), i...]
where the time goes in v3:
time: 22.3 us; the launch traced here: 22.1 us
  Pallas kernels  21.5 us (96%)
  between operations  0.64 us (3%)
    pallas_call x1, Pallas kernels, per_device(): pl.pallas_call(functools.partial(kernel, S, R), out_shape=(held, held), i...  20.8 us
    pallas_call x1, Pallas kernels, per_device(): pl.pallas_call(finish, out_shape=(done, done), in_specs=[vmem] * 2, out_s...  0.67 us

profile of v3, /device:TPU:0, one launch (start us, length us, event | category | flops | bytes accessed | tf_op | source)
XLA Modules:
  0.0 22.1 jit_solution(11683897291434945286)
XLA Ops:
  0.6 20.8 %shard_map.104 = (f32[16,1024]{1,0:T(8,128)S(1)}, f32[16,1024]{1,0:T(8,128)S(1)}) custom-call(f32[1,16,1024]{2,1,0:T(8,128)} %loads.1, f32[1,1024]{1,0:T(1,128)} %weights.1, bf16[1,1024,2048]{2,1,0:T(8,128)(2,1)} %op.1, bf16[1,24,1024]{2,1,0:T(8,128)(2,1)} %cm.1, f32[48,48]{1,0:T(8,128)} %cinv.1, s32[4,24]{1,0:T(4,128)} %ids.1, s32[4]{0:T(128)} %sizes.1, ...), custom_call_target="tpu_custom_call" | custom-call | tf_op jit(solution)/shard_map/pallas_call | solution.py:423
  21.5 0.7 %shard_map.105 = (f32[1,16,1024]{2,1,0:T(8,128)}, f32[1,16,1024]{2,1,0:T(8,128)}) custom-call(f32[16,1024]{1,0:T(8,128)S(1)} %get-tuple-element.4.a, f32[16,1024]{1,0:T(8,128)S(1)} %get-tuple-element.5.b), custom_call_target="tpu_custom_call" | custom-call | tf_op jit(solution)/shard_map/pallas_call | solution.py:448

commit v4 on v3

--- a/solution.py
+++ b/solution.py
@@ -44,7 +44,7 @@
     C, H = loads_v.shape
     B = op_v.shape[0]
     NC = cv.shape[0]
-    W = cinv_p.shape[0]
+    W = cinv_p.shape[1]
     half_r = R // 2
     nxt = lax.rem(s + 1, S)
     prv = lax.rem(s + S - 1, S)
@@ -169,8 +169,11 @@
     hot(hots.at[0], left_map)
     ins[5].wait()
     ins[6].wait()
+    c_hi = cv[...].astype(BF).astype(F32)
     cinv_p[...] = jnp.zeros_like(cinv_p)
-    cinv_p[0:NC, 0:NC] = cv[...]
+    cinv_p[0:NC, 0:NC] = c_hi
+    cinv_p[W : W + NC, 0:NC] = c_hi
+    cinv_p[2 * W : 2 * W + NC, 0:NC] = cv[...] - c_hi
 
     pl.semaphore_wait(ready.at[0], R - 1)
     pl.when(far)(lambda: launch(cm_sides[1:]))
@@ -198,15 +201,8 @@
     w_copy.wait_recv()
     for k in range(1, R):
         tell(ready.at[1], k)
-    w_in = wrecv[...]
-    w_hi = w_in.astype(BF)
-    w_lo = (w_in - w_hi.astype(F32)).astype(BF)
-    pad = lax.broadcasted_iota(jnp.int32, (16, H), 0)
-    w_rows = jnp.where(pad == 0, w_hi.astype(F32), jnp.where(pad == 1, w_lo.astype(F32), 0.0))
-    gathered = dot_nn(jnp.concatenate([zrecv[...], w_rows.astype(BF)], axis=0), hots[1])
-    z0_r = gathered[:C]
+    z0_r = dot_nn(zrecv[...], hots[1])
     zz[1] = z0_r
-    wt[1] = gathered[C : C + 1] + gathered[C + 1 : C + 2]
 
     col = lax.broadcasted_iota(jnp.int32, (C, W), 1)
     cold = lax.broadcasted_iota(jnp.int32, (C, 128), 1)
@@ -267,25 +263,23 @@
         sides = [to_side(mine, nbr, blk_ssem.at[step], nbr_rsem.at[step, k], k) for k in range(R)]
         rows = [to_row(mine, blocks.at[step], blk_ssem.at[step], own_rsem.at[step, k - 1], k) for k in range(1, R)]
 
-        spread(step, pk, pk_ssem, pk_rsem)
         if step == 0:
+            spread(step, pk, pk_ssem, pk_rsem)
             launch(rows)
-        else:
-            pl.when(side == 0)(lambda: launch(rows))
-        if step == 0:
             pl.semaphore_wait(ready.at[1], R - 1)
-        spread(step, dk, dk_ssem, dk_rsem)
-        if step == 0:
+            spread(step, dk, dk_ssem, dk_rsem)
             launch(sides)
         else:
+            spread(step, pk, pk_ssem, pk_rsem)
+            pl.when(side == 0)(lambda: launch(rows))
+            spread(step, dk, dk_ssem, dk_rsem)
             pl.when(side == 1)(lambda: launch(sides[1:] + sides[:1]))
 
     def solve(step):
         total = unpacked(gathered_sum(step, pk, pk_ssem, pk_rsem, jnp.zeros(pk.shape[2:], F32)))
-        solved = lax.dot_general(
-            total, cinv_p[...], (((1,), (0,)), ((), ())),
-            precision=lax.Precision.HIGHEST, preferred_element_type=F32,
-        )
+        t_hi = total.astype(BF)
+        t_lo = (total - t_hi.astype(F32)).astype(BF)
+        solved = dot_nn(jnp.concatenate([t_hi, t_lo, t_hi], axis=1), cinv_p[...].astype(BF))
         back = solved.astype(BF)
         gamma = pick(total, NC)
         bend = jnp.sum(total * back.astype(F32), axis=1, keepdims=True)
@@ -323,6 +317,13 @@
     local0 = acc[...] + dot_nn(z0_r.astype(BF), turned[1])
     product(0, local0, r0, z0)
 
+    w_in = wrecv[...]
+    w_hi = w_in.astype(BF)
+    w_lo = (w_in - w_hi.astype(F32)).astype(BF)
+    pad = lax.broadcasted_iota(jnp.int32, (16, H), 0)
+    w_rows = jnp.where(pad == 0, w_hi.astype(F32), jnp.where(pad == 1, w_lo.astype(F32), 0.0))
+    w_turned = dot_nn(w_rows.astype(BF), hots[1])
+    wt[1] = w_turned[0:1] + w_turned[1:2]
     hot_next = hot_ids(nxt)
     hot_prev = hot_ids(prv)
     for k in range(R):
@@ -427,7 +428,7 @@
         out_specs=(vmem, vmem),
         scratch_shapes=[
             pltpu.VMEM((C, H), F32), pltpu.VMEM((1, H), F32), pltpu.VMEM((B, full), BF),
-            pltpu.VMEM((NC, NC), F32), pltpu.VMEM((W, W), F32), pltpu.VMEM(corner_ids.shape, jnp.int32),
+            pltpu.VMEM((NC, NC), F32), pltpu.VMEM((3 * W, W), F32), pltpu.VMEM(corner_ids.shape, jnp.int32),
             pltpu.VMEM((1, H), jnp.int32), pltpu.VMEM((1, H), jnp.int32), pltpu.SMEM(iface_sizes.shape, jnp.int32),
             pltpu.VMEM((C, H), BF), pltpu.VMEM((C, H), BF), pltpu.VMEM((1, H), F32),
             pltpu.VMEM((J, B), BF), pltpu.VMEM((R,) + fold, BF), pltpu.VMEM((R,) + fold, BF),

time: 22.3 us -> 22.1 us (level)
  no operation moved by 1% of the time
where the time goes in v4:
time: 22.1 us; the launch traced here: 21.9 us
  Pallas kernels  21.3 us (96%)
  between operations  0.64 us (3%)
    pallas_call x1, Pallas kernels, per_device(): pl.pallas_call(functools.partial(kernel, S, R), out_shape=(held, held), i...  20.6 us
    pallas_call x1, Pallas kernels, per_device(): pl.pallas_call(finish, out_shape=(done, done), in_specs=[vmem] * 2, out_s...  0.67 us

profile of v4, /device:TPU:0, one launch (start us, length us, event | category | flops | bytes accessed | tf_op | source)
XLA Modules:
  0.0 21.9 jit_solution(1263401688471060684)
XLA Ops:
  0.6 20.6 %shard_map.104 = (f32[16,1024]{1,0:T(8,128)S(1)}, f32[16,1024]{1,0:T(8,128)S(1)}) custom-call(f32[1,16,1024]{2,1,0:T(8,128)} %loads.1, f32[1,1024]{1,0:T(1,128)} %weights.1, bf16[1,1024,2048]{2,1,0:T(8,128)(2,1)} %op.1, bf16[1,24,1024]{2,1,0:T(8,128)(2,1)} %cm.1, f32[48,48]{1,0:T(8,128)} %cinv.1, s32[4,24]{1,0:T(4,128)} %ids.1, s32[4]{0:T(128)} %sizes.1, ...), custom_call_target="tpu_custom_call" | custom-call | tf_op jit(solution)/shard_map/pallas_call | solution.py:424
  21.3 0.7 %shard_map.105 = (f32[1,16,1024]{2,1,0:T(8,128)}, f32[1,16,1024]{2,1,0:T(8,128)}) custom-call(f32[16,1024]{1,0:T(8,128)S(1)} %get-tuple-element.4.a, f32[16,1024]{1,0:T(8,128)S(1)} %get-tuple-element.5.b), custom_call_target="tpu_custom_call" | custom-call | tf_op jit(solution)/shard_map/pallas_call | solution.py:449

commit v5 on v4

--- a/solution.py
+++ b/solution.py
@@ -263,12 +263,21 @@
         sides = [to_side(mine, nbr, blk_ssem.at[step], nbr_rsem.at[step, k], k) for k in range(R)]
         rows = [to_row(mine, blocks.at[step], blk_ssem.at[step], own_rsem.at[step, k - 1], k) for k in range(1, R)]
 
+        def slopes(last):
+            for ds in range(S):
+                for dr in range(R):
+                    distant = 1 < ds < S - 1 and dr > 0
+                    if ds + dr > 0 and distant == last:
+                        who = {"sub": lax.rem(s + ds, S), "row": lax.rem(r + dr, R)}
+                        remote(dk.at[0, me], dk.at[0, me], dk_ssem.at[0], dk_rsem.at[0], who).start()
+
         if step == 0:
             spread(step, pk, pk_ssem, pk_rsem)
             launch(rows)
+            slopes(False)
+            launch(sides[1:] + sides[:1])
             pl.semaphore_wait(ready.at[1], R - 1)
-            spread(step, dk, dk_ssem, dk_rsem)
-            launch(sides)
+            slopes(True)
         else:
             spread(step, pk, pk_ssem, pk_rsem)
             pl.when(side == 0)(lambda: launch(rows))

time: 22.1 us -> 21.9 us (level)
  no operation moved by 1% of the time
where the time goes in v5:
time: 21.9 us; the launch traced here: 21.7 us
  Pallas kernels  21.1 us (96%)
  between operations  0.64 us (3%)
    pallas_call x1, Pallas kernels, per_device(): pl.pallas_call(functools.partial(kernel, S, R), out_shape=(held, held), i...  20.4 us
    pallas_call x1, Pallas kernels, per_device(): pl.pallas_call(finish, out_shape=(done, done), in_specs=[vmem] * 2, out_s...  0.67 us

profile of v5, /device:TPU:0, one launch (start us, length us, event | category | flops | bytes accessed | tf_op | source)
XLA Modules:
  0.0 21.7 jit_solution(10328686988664840591)
XLA Ops:
  0.6 20.4 %shard_map.104 = (f32[16,1024]{1,0:T(8,128)S(1)}, f32[16,1024]{1,0:T(8,128)S(1)}) custom-call(f32[1,16,1024]{2,1,0:T(8,128)} %loads.1, f32[1,1024]{1,0:T(1,128)} %weights.1, bf16[1,1024,2048]{2,1,0:T(8,128)(2,1)} %op.1, bf16[1,24,1024]{2,1,0:T(8,128)(2,1)} %cm.1, f32[48,48]{1,0:T(8,128)} %cinv.1, s32[4,24]{1,0:T(4,128)} %ids.1, s32[4]{0:T(128)} %sizes.1, ...), custom_call_target="tpu_custom_call" | custom-call | tf_op jit(solution)/shard_map/pallas_call | solution.py:433
  21.1 0.7 %shard_map.105 = (f32[1,16,1024]{2,1,0:T(8,128)}, f32[1,16,1024]{2,1,0:T(8,128)}) custom-call(f32[16,1024]{1,0:T(8,128)S(1)} %get-tuple-element.4.a, f32[16,1024]{1,0:T(8,128)S(1)} %get-tuple-element.5.b), custom_call_target="tpu_custom_call" | custom-call | tf_op jit(solution)/shard_map/pallas_call | solution.py:458

commit v6 on v5

--- a/solution.py
+++ b/solution.py
@@ -35,7 +35,7 @@
     zsend, zrecv, wrecv, cm_v, cmo, cmn, mm, hots, zs, acc, turned, zz, wt, live, fixed, met,
     blocks, pk, dk,
     in_sem, op_sem, z_sem, cmo_ssem, cmo_rsem, cmn_ssem, cmn_rsem,
-    blk_ssem, own_rsem, nbr_rsem, pk_ssem, pk_rsem, dk_ssem, dk_rsem, ready,
+    blk_ssem, own_rsem, nbr_rsem, pk_ssem, pk_rsem, dk_ssem, dk_rsem, ready, led,
 ):
     s = lax.axis_index("sub")
     r = lax.axis_index("row")
@@ -196,6 +196,12 @@
         q = lax.rem(r + R - k, R)
         wait_slot(cmo, cmo_rsem.at[k - 1], q)
         mm[q, 0:W] = spreadout(hot_own, cmo[q]).astype(BF)
+    lead = jnp.where(
+        lax.broadcasted_iota(jnp.int32, (C, W), 1) == NC, jnp.sum(r0 * z0, axis=1, keepdims=True), 0.0
+    )
+    for q in range(half_r):
+        lead = lead + dot_nt(z0[:, q * B : (q + 1) * B].astype(BF), mm[q, 0:W])
+    led[...] = lead
     pl.when(jnp.logical_not(far))(lambda: launch(cm_sides[1:]))
     z_copy.wait_recv()
     w_copy.wait_recv()
@@ -254,9 +260,12 @@
         mine = blocks.at[step, r]
         delta = jnp.sum(zs[r] * local, axis=1, keepdims=True)
         dk[step, me] = jnp.sum(jnp.where(diag, delta, 0.0), axis=0, keepdims=True)
-        gamma = jnp.sum(r_left * z_left, axis=1, keepdims=True)
-        corner = jnp.where(col == NC, gamma, 0.0)
-        for q in range(R):
+        if step == 0:
+            corner = led[...]
+        else:
+            gamma = jnp.sum(r_left * z_left, axis=1, keepdims=True)
+            corner = jnp.where(col == NC, gamma, 0.0)
+        for q in range(half_r if step == 0 else 0, R):
             corner = corner + dot_nt(zs[q].astype(BF), mm[q, 0:W])
         pk[step, s] = packed(corner)
         nbr = blocks.at[step, pl.ds(R, R)]
@@ -294,9 +303,9 @@
         bend = jnp.sum(total * back.astype(F32), axis=1, keepdims=True)
         return back, gamma, bend
 
-    def bent(back, first, last):
+    def bent(back, first, count):
         twice = jnp.concatenate([back, back], axis=1)
-        return jnp.concatenate([dot_nn(twice, mm[q]) for q in range(first, last)], axis=1)
+        return jnp.concatenate([dot_nn(twice, mm[first + j]) for j in range(count)], axis=1)
 
     def slope(step, total, bend):
         return jnp.sum(jnp.where(diag, total, 0.0), axis=1, keepdims=True) + bend
@@ -351,11 +360,12 @@
     meet(0, early)
     met[early] = meeting(0, early)
     back0, gamma0, bend0 = solve(0)
-    fixed[0] = bent(back0, 0, half_r)
-    fixed[1] = bent(back0, half_r, R)
+    fixed[early] = bent(back0, early * half_r, half_r)
     steep0 = gathered_sum(0, dk, dk_ssem, dk_rsem, jnp.zeros((1, 128), F32))
     delta0 = slope(0, steep0, bend0)
     alpha0 = gamma0 / delta0
+
+    fixed[late] = bent(back0, late * half_r, half_r)
 
     def advance(d):
         met[d] = (met[d] + fixed[d]) * live[d]
@@ -448,7 +458,7 @@
             pltpu.VMEM((2, 2 * R, C, B), BF), pltpu.VMEM((2, S, 8 if C == 16 and W == 128 and NC < 64 else C, W), F32),
             pltpu.VMEM((2, G, 1, 128), F32),
             DMA((8,)), DMA, DMA((4,)), DMA((R - 1,)), DMA((R - 1,)), DMA((R,)), DMA((R,)),
-            DMA((2,)), DMA((2, R - 1)), DMA((2, R)), DMA((2,)), DMA((2,)), DMA((2,)), DMA((2,)), pltpu.SemaphoreType.REGULAR((2,)),
+            DMA((2,)), DMA((2, R - 1)), DMA((2, R)), DMA((2,)), DMA((2,)), DMA((2,)), DMA((2,)), pltpu.SemaphoreType.REGULAR((2,)), pltpu.VMEM((C, W), F32),
         ],
         compiler_params=pltpu.CompilerParams(
             collective_id=0, has_side_effects=True, vmem_limit_bytes=LIMIT

time: 21.9 us -> 22 us (level)
  no operation moved by 1% of the time
where the time goes in v6:
time: 22 us; the launch traced here: 21.8 us
  Pallas kernels  21.2 us (96%)
  between operations  0.64 us (3%)
    pallas_call x1, Pallas kernels, per_device(): pl.pallas_call(functools.partial(kernel, S, R), out_shape=(held, held), i...  20.5 us
    pallas_call x1, Pallas kernels, per_device(): pl.pallas_call(finish, out_shape=(done, done), in_specs=[vmem] * 2, out_s...  0.67 us

profile of v6, /device:TPU:0, one launch (start us, length us, event | category | flops | bytes accessed | tf_op | source)
XLA Modules:
  0.0 21.8 jit_solution(10457639107432276746)
XLA Ops:
  0.6 20.5 %shard_map.104 = (f32[16,1024]{1,0:T(8,128)S(1)}, f32[16,1024]{1,0:T(8,128)S(1)}) custom-call(f32[1,16,1024]{2,1,0:T(8,128)} %loads.1, f32[1,1024]{1,0:T(1,128)} %weights.1, bf16[1,1024,2048]{2,1,0:T(8,128)(2,1)} %op.1, bf16[1,24,1024]{2,1,0:T(8,128)(2,1)} %cm.1, f32[48,48]{1,0:T(8,128)} %cinv.1, s32[4,24]{1,0:T(4,128)} %ids.1, s32[4]{0:T(128)} %sizes.1, ...), custom_call_target="tpu_custom_call" | custom-call | tf_op jit(solution)/shard_map/pallas_call | solution.py:443
  21.1 0.7 %shard_map.105 = (f32[1,16,1024]{2,1,0:T(8,128)}, f32[1,16,1024]{2,1,0:T(8,128)}) custom-call(f32[16,1024]{1,0:T(8,128)S(1)} %get-tuple-element.4.a, f32[16,1024]{1,0:T(8,128)S(1)} %get-tuple-element.5.b), custom_call_target="tpu_custom_call" | custom-call | tf_op jit(solution)/shard_map/pallas_call | solution.py:468
